TPU v7x, 32 devices: a whole 2x2x4 slice. The times are simulated.
32 devices in a mesh: mats: 8 (over z, x), tp: 4 (over y, core).
Axes of the slice: x: 2, y: 2, z: 4, core: 2. Of those that a mesh axis runs over, the one named last changes fastest.
Arguments:
- grad: bfloat16 [3072, 16384], P('tp', 'mats'), may hold values from -40 to 40
- momentum: float32 [3072, 16384], P('tp', 'mats'), may hold values from -6 to 6
Outputs:
- update: bfloat16 [3072, 16384], P('tp', 'mats')
- new_momentum: float32 [3072, 16384], P('tp', 'mats')
All inputs are finite; a program needn't handle non-finite values.
Results may differ from a plain program's by a relative error of at most 0.01.
Values may be sent and summed in bfloat16 or wider, within the bound.
A program may use at most 128 MiB of HBM per device.

v0:
```python
import math

import jax
import jax.numpy as jnp
from jax import lax
from jax.sharding import PartitionSpec as P

R = 3072
C = 16384
ITERS = 2


momentum_beta = 0.95
first_coef = 3.4445
second_coef = -4.775
third_coef = 2.0315
shape_gain = 0.2
epsilon = 1e-06


def row_dot(left, right):
    return lax.dot_general(
        left, right, (((1,), (1,)), ((), ())), preferred_element_type=jnp.float32
    )


def per_device(grad, momentum):
    new_momentum = momentum_beta * momentum + grad.astype(jnp.float32)
    iterate = (grad.astype(jnp.float32) + momentum_beta * new_momentum).astype(jnp.bfloat16)
    for step in range(ITERS):
        columns = lax.all_gather(iterate, "tp", axis=0, tiled=True)
        block = iterate
        share = lax.psum_scatter(
            row_dot(block, columns), "mats", scatter_dimension=0, tiled=True
        ).astype(jnp.bfloat16)
        gram = lax.all_gather(share, "mats", axis=0, tiled=True)
        if step == 0:
            local_peak = jnp.max(jnp.sum(jnp.abs(gram.astype(jnp.float32)), axis=1))
            bound = lax.pmax(local_peak, "tp") + epsilon
            root = lax.rsqrt(bound)
        first = jnp.dot(gram, columns, preferred_element_type=jnp.float32).astype(jnp.bfloat16)
        second = jnp.dot(
            gram,
            lax.all_gather(first, "tp", axis=0, tiled=True),
            preferred_element_type=jnp.float32,
        ).astype(jnp.bfloat16)
        if step == 0:
            mixed = (
                first_coef * iterate.astype(jnp.float32) * root
                + second_coef * first.astype(jnp.float32) * root**3
                + third_coef * second.astype(jnp.float32) * root**5
            )
        else:
            mixed = (
                first_coef * iterate.astype(jnp.float32)
                + second_coef * first.astype(jnp.float32)
                + third_coef * second.astype(jnp.float32)
            )
        iterate = mixed.astype(jnp.bfloat16)
    update = (shape_gain * math.sqrt(max(R, C)) * iterate.astype(jnp.float32)).astype(jnp.bfloat16)
    return (update, new_momentum)


def solution(mesh):
    in_specs = (P("tp", "mats"), P("tp", "mats"))
    out_specs = (P("tp", "mats"), P("tp", "mats"))
    return jax.shard_map(
        per_device, mesh=mesh, in_specs=in_specs, out_specs=out_specs, check_vma=False
    )
```

profile of v0, /device:TPU:0, one launch (start us, length us, event | category | flops | bytes accessed | tf_op | source)
XLA Modules:
  0.0 933.5 jit_solution(4649646977199334676)
XLA Ops:
  7.2 9.3 fusion
  16.5 0.0 reduce-scatter.3.cloned.1.call-start
  16.5 84.9 %all-gather.7.cloned.1.call-done = bf16[3072,2048]{1,0:T(8,128)(2,1)} async-done(((bf16[768,2048]{1,0:T(8,128)(2,1)}), bf16[3072,2048]{1,0:T(8,128)(2,1)}) %all-gather.7.cloned.1.call-update) | async-done | bytes 12582928 | tf_op jit(solution)/shard_map/all_gather | solution.py:31
  101.5 16.0 %fusion.1 = f32[768,3072]{1,0:T(8,128)} fusion(bf16[768,2048]{1,0:T(8,128)(2,1)} %get-tuple-element.2, bf16[3072,2048]{1,0:T(8,128)(2,1)} %all-gather.7.cloned.1.call-done), kind=kOutput, calls=%fused_computation.11 | convolution fusion | flops 9663676416 | bytes 25165824 | tf_op jit(solution)/shard_map/dot_general | solution.py:22
  117.5 162.2 %reduce-scatter.3.cloned.1.call-done = f32[96,3072]{1,0:T(8,128)} async-done(((f32[768,3072]{1,0:T(8,128)}), f32[96,3072]{1,0:T(8,128)}) %reduce-scatter.3.cloned.1.call-update) | async-done | bytes 1179664 | tf_op jit(solution)/shard_map/reduce_scatter | solution.py:33
  279.8 2.2 convert_element_type.61
  281.9 0.0 all-gather.11.cloned.1.call-start
  282.0 78.5 %all-gather.9.cloned.1.call-done = bf16[768,3072]{1,0:T(8,128)(2,1)} async-done(((bf16[96,3072]{1,0:T(8,128)(2,1)}), bf16[768,3072]{1,0:T(8,128)(2,1)}) %all-gather.9.cloned.1.call-update) | async-done | bytes 4718608 | tf_op jit(solution)/shard_map/all_gather | solution.py:36
  360.5 15.4 %convolution_convert_fusion.3 = bf16[768,2048]{1,0:T(8,128)(2,1)} fusion(bf16[768,3072]{1,0:T(8,128)(2,1)} %all-gather.9.cloned.1.call-done, bf16[3072,2048]{1,0:T(8,128)(2,1)} %all-gather.7.cloned.1.call-done), kind=kOutput, calls=%fused_computation.10 | convolution fusion | flops 9665249280 | bytes 20447232 | tf_op jit(solution)/shard_map/dot_general | solution.py:41
  376.0 3.5 abs_reduce_fusion
  379.5 0.6 reduce_max.9
  380.1 6.5 pmax.7
  387.3 69.3 %all-gather.11.cloned.1.call-done = bf16[3072,2048]{1,0:T(8,128)(2,1)} async-done(((bf16[768,2048]{1,0:T(8,128)(2,1)}), bf16[3072,2048]{1,0:T(8,128)(2,1)}) %all-gather.11.cloned.1.call-update) | async-done | bytes 12582928 | tf_op jit(solution)/shard_map/all_gather | solution.py:44
  456.6 16.2 %add_convert_fusion.1 = bf16[768,2048]{1,0:T(8,128)(2,1)} fusion(bf16[768,2048]{1,0:T(8,128)(2,1)} %convolution_convert_fusion.3, bf16[768,2048]{1,0:T(8,128)(2,1)S(1)} %copy-done, bf16[768,3072]{1,0:T(8,128)(2,1)} %all-gather.9.cloned.1.call-done, bf16[3072,2048]{1,0:T(8,128)(2,1)} %all-gather.11.cloned.1.call-done, f32[]{:T(128)S(6)} %mul.65, ...), kind=kOutput, calls=%fused_computation.6 | convolution fusion | flops 9679405056 | bytes 26738700 | tf_op jit(solution)/shard_map/dot_general | solution.py:42
  472.9 82.2 %all-gather.13.cloned.1.call-done = bf16[3072,2048]{1,0:T(8,128)(2,1)} async-done(((bf16[768,2048]{1,0:T(8,128)(2,1)}), bf16[3072,2048]{1,0:T(8,128)(2,1)}) %all-gather.13.cloned.1.call-update) | async-done | bytes 12582928 | tf_op jit(solution)/shard_map/all_gather | solution.py:31
  555.1 16.0 %fusion.2 = f32[768,3072]{1,0:T(8,128)} fusion(bf16[768,2048]{1,0:T(8,128)(2,1)} %add_convert_fusion.1, bf16[3072,2048]{1,0:T(8,128)(2,1)} %all-gather.13.cloned.1.call-done), kind=kOutput, calls=%fused_computation.12 | convolution fusion | flops 9663676416 | bytes 25165824 | tf_op jit(solution)/shard_map/dot_general | solution.py:22
  571.1 0.0 all-gather.15.cloned.1.call-start
  571.2 162.2 %reduce-scatter.5.cloned.1.call-done = f32[96,3072]{1,0:T(8,128)} async-done(((f32[768,3072]{1,0:T(8,128)}), f32[96,3072]{1,0:T(8,128)}) %reduce-scatter.5.cloned.1.call-update) | async-done | bytes 1179664 | tf_op jit(solution)/shard_map/reduce_scatter | solution.py:33
  733.4 2.2 convert_element_type.69
  735.6 0.3 all-gather.17.cloned.1.call-start
  735.8 78.3 %all-gather.15.cloned.1.call-done = bf16[768,3072]{1,0:T(8,128)(2,1)} async-done(((bf16[96,3072]{1,0:T(8,128)(2,1)}), bf16[768,3072]{1,0:T(8,128)(2,1)}) %all-gather.15.cloned.1.call-update) | async-done | bytes 4718608 | tf_op jit(solution)/shard_map/all_gather | solution.py:36
  814.1 15.4 %convolution_convert_fusion.1 = bf16[768,2048]{1,0:T(8,128)(2,1)} fusion(bf16[768,3072]{1,0:T(8,128)(2,1)} %all-gather.15.cloned.1.call-done, bf16[3072,2048]{1,0:T(8,128)(2,1)} %all-gather.13.cloned.1.call-done), kind=kOutput, calls=%fused_computation.8 | convolution fusion | flops 9665249280 | bytes 20447232 | tf_op jit(solution)/shard_map/dot_general | solution.py:41
  829.5 80.6 %all-gather.17.cloned.1.call-done = bf16[3072,2048]{1,0:T(8,128)(2,1)} async-done(((bf16[768,2048]{1,0:T(8,128)(2,1)}), bf16[3072,2048]{1,0:T(8,128)(2,1)}) %all-gather.17.cloned.1.call-update) | async-done | bytes 12582928 | tf_op jit(solution)/shard_map/all_gather | solution.py:44
  910.2 16.5 %multiply_convert_fusion = bf16[768,2048]{1,0:T(8,128)(2,1)} fusion(bf16[768,3072]{1,0:T(8,128)(2,1)} %all-gather.15.cloned.1.call-done, bf16[3072,2048]{1,0:T(8,128)(2,1)} %all-gather.17.cloned.1.call-done, bf16[768,2048]{1,0:T(8,128)(2,1)} %convolution_convert_fusion.1, bf16[768,2048]{1,0:T(8,128)(2,1)S(1)} %copy-done.1), kind=kOutput, calls=%fused_computation.4 | convolution fusion | flops 9684123648 | bytes 26738688 | tf_op jit(solution)/shard_map/dot_general | solution.py:42
  (16 shorter events, 0.3 us)
Async XLA Ops:
  7.2 94.3 %all-gather.7.cloned.1.call-start = ((), (), s32[]{:S(2)}) async-start(), calls=%async_computation.2 | async-start | bytes 15728640 | tf_op jit(solution)/shard_map/all_gather | solution.py:31
  16.5 263.3 %reduce-scatter.3.cloned.1.call-start = ((), (), s32[]{:S(2)}) async-start(), calls=%async_computation.3 | async-start | bytes 10616832 | tf_op jit(solution)/shard_map/reduce_scatter | solution.py:33
  117.5 243.0 %all-gather.9.cloned.1.call-start = ((), (), s32[]{:S(2)}) async-start(), calls=%async_computation.4 | async-start | bytes 5308416 | tf_op jit(solution)/shard_map/all_gather | solution.py:36
  281.9 174.6 %all-gather.11.cloned.1.call-start = ((), (), s32[]{:S(2)}) async-start(), calls=%async_computation.5 | async-start | bytes 15728640 | tf_op jit(solution)/shard_map/all_gather | solution.py:44
  375.9 80.6 %copy-start = (bf16[768,2048]{1,0:T(8,128)(2,1)S(1)}, bf16[768,2048]{1,0:T(8,128)(2,1)}, u32[]{:S(2)}) copy-start(bf16[768,2048]{1,0:T(8,128)(2,1)} %get-tuple-element.2) | copy-start | bytes 9437188
  376.0 179.1 %all-gather.13.cloned.1.call-start = ((), (), s32[]{:S(2)}) async-start(), calls=%async_computation.6 | async-start | bytes 15728640 | tf_op jit(solution)/shard_map/all_gather | solution.py:31
  472.8 260.5 %reduce-scatter.5.cloned.1.call-start = ((), (), s32[]{:S(2)}) async-start(), calls=%async_computation.7 | async-start | bytes 10616832 | tf_op jit(solution)/shard_map/reduce_scatter | solution.py:33
  571.1 243.0 %all-gather.15.cloned.1.call-start = ((), (), s32[]{:S(2)}) async-start(), calls=%async_computation.8 | async-start | bytes 5308416 | tf_op jit(solution)/shard_map/all_gather | solution.py:36
  735.5 174.6 %copy-start.1 = (bf16[768,2048]{1,0:T(8,128)(2,1)S(1)}, bf16[768,2048]{1,0:T(8,128)(2,1)}, u32[]{:S(2)}) copy-start(bf16[768,2048]{1,0:T(8,128)(2,1)} %add_convert_fusion.1) | copy-start | bytes 9437188
  735.6 174.6 %all-gather.17.cloned.1.call-start = ((), (), s32[]{:S(2)}) async-start(), calls=%async_computation.9 | async-start | bytes 15728640 | tf_op jit(solution)/shard_map/all_gather | solution.py:44
Sparse Core Ops, SparseCore 0:
  16.6 84.7 all-gather.6
  117.6 162.0 reduce-scatter.2
  282.1 78.4 all-gather.8
  376.1 80.4 all-gather.10
  472.9 82.0 all-gather.12
  571.2 162.0 reduce-scatter.4
  735.7 78.3 all-gather.14
  829.7 80.4 all-gather.16
where the time goes:
time: 934 us; the launch traced here: 933 us
  waiting for transfers between devices  798 us (85%)
  matrix products  95.6 us (10%)
  other arithmetic  17.7 us (2%)
  between operations  14.8 us (2%)
    reduce_scatter x2, waiting for transfers between devices, per_device(): lax.psum_scatter(row_dot(block, columns), 'mats', scatter_dimension=0, ti...  324 us
    all_gather x2, waiting for transfers between devices, per_device(): columns = lax.all_gather(iterate, 'tp', axis=0, tiled=True)  167 us
    all_gather x2, waiting for transfers between devices, per_device(): gram = lax.all_gather(share, 'mats', axis=0, tiled=True)  157 us
    all_gather x2, waiting for transfers between devices, per_device(): lax.all_gather(first, 'tp', axis=0, tiled=True)  150 us
    dot_general x2, matrix products, per_device(): jnp.dot(gram, lax.all_gather(first, 'tp', axis=0, tiled=True), preferred_...  32.7 us
    dot_general x2, matrix products, row_dot(): lax.dot_general(left, right, (((1,), (1,)), ((), ())), preferred_element_...  32 us
    dot_general x2, matrix products, per_device(): jnp.dot(gram, columns, preferred_element_type=jnp.float32)  30.8 us
  transfers between devices with their start and end apart: 8, of which 8 were waited for; matrix products, arithmetic and copies ran while one was open for 0% of the time, Pallas kernels for 0%

commit v1 on v0

v1 whole, which is shorter than its diff:
```python
import functools
import math

import jax
import jax.numpy as jnp
from jax import lax
from jax.experimental import pallas as pl
from jax.experimental.pallas import tpu as pltpu
from jax.sharding import PartitionSpec as P

momentum_beta = 0.95
first_coef = 3.4445
second_coef = -4.775
third_coef = 2.0315
shape_gain = 0.2
epsilon = 1e-06


def row_dot(left, right):
    return lax.dot_general(
        left, right, (((1,), (1,)), ((), ())), preferred_element_type=jnp.float32
    )


def chain_kernel(tile, scale, bound_ref, gram_ref, x_ref, out_ref, base, held, left, right, saved):
    rows = x_ref.shape[0]
    bound = bound_ref[0, 0]
    root = lax.rsqrt(jnp.full((1, x_ref.shape[1]), bound, jnp.float32))
    inverse = root * root

    def tiles(body):
        @pl.loop(0, rows // tile)
        def _(step):
            body(pl.ds(pl.multiple_of(step * tile, tile), tile))

    def product(at, source):
        return inverse * jnp.dot(
            gram_ref[at, :], source[...], preferred_element_type=jnp.float32
        )

    def apply(source, target):
        def body(at):
            target[at, :] = product(at, source).astype(jnp.bfloat16)

        tiles(body)

    def combine(at, zeroth, once, twice):
        return (
            first_coef * zeroth[at, :].astype(jnp.float32)
            + second_coef * once[at, :].astype(jnp.float32)
            + third_coef * twice
        )

    def polynomial(source, target):
        apply(source, left)

        def body(at):
            target[at, :] = combine(at, source, left, product(at, left)).astype(jnp.bfloat16)

        tiles(body)

    def normalize(at):
        right[at, :] = (x_ref[at, :].astype(jnp.float32) * root).astype(jnp.bfloat16)

    tiles(normalize)
    polynomial(right, base)

    def start(at):
        held[at, :] = base[at, :]

    tiles(start)

    @pl.loop(0, 2)
    def _(turn):
        polynomial(held, right)
        polynomial(right, right)
        apply(right, held)

        @pl.when(turn == 0)
        def _():
            def keep(at):
                saved[at, :] = held[at, :]

            tiles(keep)

    def finish(at):
        mixed = combine(at, base, saved, held[at, :].astype(jnp.float32)).astype(jnp.bfloat16)
        out_ref[at, :] = (scale * mixed.astype(jnp.float32)).astype(jnp.bfloat16)

    tiles(finish)


def per_device(scale, grad, momentum):
    new_momentum = momentum_beta * momentum + grad.astype(jnp.float32)
    iterate = (grad.astype(jnp.float32) + momentum_beta * new_momentum).astype(jnp.bfloat16)
    columns = lax.all_gather(iterate, "tp", axis=0, tiled=True)
    part = row_dot(iterate, columns).astype(jnp.bfloat16)
    share = lax.psum_scatter(part, "mats", scatter_dimension=0, tiled=True)
    peak = jnp.max(jnp.sum(jnp.abs(share.astype(jnp.float32)), axis=1))
    bound = lax.pmax(peak, ("tp", "mats")) + epsilon
    gram = lax.all_gather(share, ("tp", "mats"), axis=0, tiled=True)
    rows = columns.shape[0]
    width = columns.shape[1] // lax.axis_size("tp")
    own = lax.dynamic_slice_in_dim(columns, lax.axis_index("tp") * width, width, axis=1)
    tile = math.gcd(rows, 512)
    whole = pl.BlockSpec(memory_space=pltpu.VMEM)
    result = pl.pallas_call(
        functools.partial(chain_kernel, tile, scale),
        out_shape=jax.ShapeDtypeStruct(own.shape, jnp.bfloat16),
        in_specs=[pl.BlockSpec(memory_space=pltpu.SMEM), whole, whole],
        out_specs=whole,
        scratch_shapes=[pltpu.VMEM(own.shape, jnp.bfloat16)] * 5,
        compiler_params=pltpu.CompilerParams(vmem_limit_bytes=60 * 1024 * 1024),
        cost_estimate=pl.CostEstimate(
            flops=24 * rows * rows * width, bytes_accessed=2 * rows * rows, transcendentals=0
        ),
    )(bound.reshape(1, 1), gram, own)
    update = lax.all_to_all(result, "tp", 0, 1, tiled=True)
    return (update, new_momentum)


def solution(mesh):
    def step(grad, momentum):
        scale = shape_gain * math.sqrt(max(grad.shape))
        return jax.shard_map(
            functools.partial(per_device, scale),
            mesh=mesh,
            in_specs=(P("tp", "mats"), P("tp", "mats")),
            out_specs=(P("tp", "mats"), P("tp", "mats")),
            check_vma=False,
        )(grad, momentum)

    return step
```

time: 934 us -> 534 us (0.57)
  waiting for transfers between devices: 798 us -> 260 us
  Pallas kernels: 0 us -> 144 us
  matrix products: 95.6 us -> 15.3 us
  blocking collectives: 6.46 us -> 82.8 us
    reduce_scatter x2 -> x1, waiting for transfers between devices: 324 us -> 96.2 us  [per_device(): share = lax.psum_scatter(part, 'mats', scatter_dimension=0, tiled=True)]
    all_gather x4 -> x1, waiting for transfers between devices: 307 us -> 78.8 us  [per_device(): gram = lax.all_gather(share, ('tp', 'mats'), axis=0, tiled=True)]
    pallas_call x0 -> x1, Pallas kernels: none -> 144 us  [per_device(): pl.pallas_call(functools.partial(chain_kernel, tile, scale), out_shape=ja...]
    all_gather x2 -> x1, waiting for transfers between devices: 167 us -> 84.9 us  [per_device(): columns = lax.all_gather(iterate, 'tp', axis=0, tiled=True)]
    dot_general x4 -> x0, matrix products: 63.5 us -> none  [the longest x2 32.7 us: per_device(): jnp.dot(gram, lax.all_gather(first, 'tp', axis=0, tiled=True), preferred_...]
    all_to_all x0 -> x1, blocking collectives: none -> 40.6 us  [per_device(): update = lax.all_to_all(result, 'tp', 0, 1, tiled=True)]
    pmax x1, blocking collectives: 6.46 us -> 42.3 us  [per_device(): bound = lax.pmax(peak, ('tp', 'mats')) + epsilon]
    dot_general x2 -> x1, matrix products: 32 us -> 15.3 us  [row_dot(): lax.dot_general(left, right, (((1,), (1,)), ((), ())), preferred_element_...]
  transfers between devices with their start and end apart: 8 -> 3, of which waited for: 8 -> 3; matrix products, arithmetic and copies ran while one was open for 0% -> 1% of each run, Pallas kernels for 0% -> 0%
where the time goes in v1:
time: 534 us; the launch traced here: 533 us
  waiting for transfers between devices  260 us (49%)
  Pallas kernels  144 us (27%)
  blocking collectives  82.8 us (16%)
  matrix products  15.3 us (3%)
  between operations  14.4 us (3%)
  other arithmetic  11.2 us (2%)
  local copies, waits for them, and re-layouts  5.9 us (1%)
    pallas_call x1, Pallas kernels, per_device(): pl.pallas_call(functools.partial(chain_kernel, tile, scale), out_shape=ja...  144 us
    reduce_scatter x1, waiting for transfers between devices, per_device(): share = lax.psum_scatter(part, 'mats', scatter_dimension=0, tiled=True)  96.2 us
    all_gather x1, waiting for transfers between devices, per_device(): columns = lax.all_gather(iterate, 'tp', axis=0, tiled=True)  84.9 us
    all_gather x1, waiting for transfers between devices, per_device(): gram = lax.all_gather(share, ('tp', 'mats'), axis=0, tiled=True)  78.8 us
    pmax x1, blocking collectives, per_device(): bound = lax.pmax(peak, ('tp', 'mats')) + epsilon  42.3 us
    all_to_all x1, blocking collectives, per_device(): update = lax.all_to_all(result, 'tp', 0, 1, tiled=True)  40.6 us
    dot_general x1, matrix products, row_dot(): lax.dot_general(left, right, (((1,), (1,)), ((), ())), preferred_element_...  15.3 us
  transfers between devices with their start and end apart: 3, of which 3 were waited for; matrix products, arithmetic and copies ran while one was open for 1% of the time, Pallas kernels for 0%

profile of v1, /device:TPU:0, one launch (start us, length us, event | category | flops | bytes accessed | tf_op | source)
XLA Modules:
  0.0 533.4 jit_solution(10666718813383570961)
XLA Ops:
  7.2 0.0 all-gather.3.cloned.1.call-start
  7.2 9.3 %fusion = (bf16[768,2048]{1,0:T(8,128)(2,1)}, f32[768,2048]{1,0:T(8,128)}) fusion(bf16[768,2048]{1,0:T(8,128)(2,1)} %param.2, f32[768,2048]{1,0:T(8,128)} %param.3), kind=kLoop, calls=%fused_computation.2 | loop fusion | flops 9437184 | bytes 18874368 | tf_op jit(solution)/shard_map/convert_element_type | solution.py:95
  16.5 0.0 all-gather.3.cloned.1.call-update
  16.5 0.0 reduce-scatter.2.cloned.1.call-start
  16.5 84.9 %all-gather.3.cloned.1.call-done = bf16[3072,2048]{1,0:T(8,128)(2,1)} async-done(((bf16[768,2048]{1,0:T(8,128)(2,1)}), bf16[3072,2048]{1,0:T(8,128)(2,1)}) %all-gather.3.cloned.1.call-update) | async-done | bytes 12582928 | tf_op jit(solution)/shard_map/all_gather | solution.py:96
  101.5 15.3 %convolution_convert_fusion = bf16[768,3072]{1,0:T(8,128)(2,1)} fusion(bf16[768,2048]{1,0:T(8,128)(2,1)} %get-tuple-element.2, bf16[3072,2048]{1,0:T(8,128)(2,1)} %all-gather.3.cloned.1.call-done), kind=kOutput, calls=%fused_computation.3 | convolution fusion | flops 9666035712 | bytes 20447232 | tf_op jit(solution)/shard_map/dot_general | solution.py:20
  116.8 0.0 reduce-scatter.2.cloned.1.call-update
  116.8 0.0 all-gather.5.cloned.1.call-start
  116.8 96.2 %reduce-scatter.2.cloned.1.call-done = bf16[96,3072]{1,0:T(8,128)(2,1)} async-done(((bf16[768,3072]{1,0:T(8,128)(2,1)}), bf16[96,3072]{1,0:T(8,128)(2,1)}) %reduce-scatter.2.cloned.1.call-update) | async-done | bytes 589840 | tf_op jit(solution)/shard_map/reduce_scatter | solution.py:98
  213.0 0.0 all-gather.5.cloned.1.call-update
  213.0 1.3 abs_reduce_fusion
  214.3 0.7 reduce_max.9
  215.0 3.8 constant_dynamic-slice_fusion.x_ref
  218.7 42.3 %pmax.7 = f32[]{:T(128)} all-reduce(f32[]{:T(128)} %reduce_max.9), channel_id=1, replica_groups=mesh['mats'=8,'tp'=4] {'tp','mats'}, use_global_device_ids=true, to_apply=%region_3.0 | all-reduce | flops 1 | bytes 8 | tf_op jit(solution)/shard_map/pmax | solution.py:100
  261.7 78.8 %all-gather.5.cloned.1.call-done.gram_ref = bf16[3072,3072]{1,0:T(8,128)(2,1)} async-done(((bf16[96,3072]{1,0:T(8,128)(2,1)}), bf16[3072,3072]{1,0:T(8,128)(2,1)}) %all-gather.5.cloned.1.call-update) | async-done | bytes 18874384 | tf_op jit(solution)/shard_map/all_gather | solution.py:101
  340.5 143.6 %shard_map.41 = bf16[3072,512]{1,0:T(8,128)(2,1)} custom-call(f32[1,1]{1,0:T(1,128)} %bitcast.bound_ref, bf16[3072,3072]{1,0:T(8,128)(2,1)} %all-gather.5.cloned.1.call-done.gram_ref, bf16[3072,512]{1,0:T(8,128)(2,1)} %constant_dynamic-slice_fusion.x_ref), custom_call_target="tpu_custom_call" | custom-call | flops 115964116992 | bytes 18874368 | tf_op jit(solution)/shard_map/pallas_call | solution.py:107
  484.2 40.6 %all_to_all.19 = bf16[4,768,512]{2,1,0:T(8,128)(2,1)S(1)} all-to-all(bf16[4,768,512]{2,1,0:T(8,128)(2,1)} %bitcast.9), channel_id=1, replica_groups=mesh['mats'=8,'tp'=4] {'tp'}, dimensions={0} | all-to-all | bytes 6291456 | tf_op jit(solution)/shard_map/all_to_all | solution.py:118
  524.7 2.1 copy.5
Async XLA Ops:
  7.2 94.3 %all-gather.3.cloned.1.call-start = ((), (), s32[]{:S(2)}) async-start(), calls=%async_computation.2 | async-start | bytes 15728640 | tf_op jit(solution)/shard_map/all_gather | solution.py:96
  16.5 196.5 %reduce-scatter.2.cloned.1.call-start = ((), (), s32[]{:S(2)}) async-start(), calls=%async_computation.3 | async-start | bytes 5308416 | tf_op jit(solution)/shard_map/reduce_scatter | solution.py:98
  116.8 223.7 %all-gather.5.cloned.1.call-start = ((), (), s32[]{:S(2)}) async-start(), calls=%async_computation.4 | async-start | bytes 19464192 | tf_op jit(solution)/shard_map/all_gather | solution.py:101
Sparse Core Ops, SparseCore 0:
  16.6 84.7 all-gather.2
  116.9 96.0 reduce-scatter.1
  216.0 124.4 all-gather.4
